TPU v7x, 32 devices: a whole 2x2x4 slice. The times are simulated.
32 devices in a mesh: groups: 2 (over y), pool: 8 (over z, x), heads: 2 (over core).
Axes of the slice: x: 2, y: 2, z: 4, core: 2. Of those that a mesh axis runs over, the one named last changes fastest.
Arguments:
- hidden_in: bfloat16 [32, 8192], P('groups'), parts along dimension 0, may hold values from -50 to 50
- key_cache: bfloat16 [32, 8, 4096, 128], P('groups', 'heads', 'pool'), parts along dimension 0, may hold values from -200 to 200
- value_cache: bfloat16 [32, 8, 4096, 128], P('groups', 'heads', 'pool'), parts along dimension 0, may hold values from -6 to 6
- positions: int32 [3, 32, 4096], P(None, 'groups', 'pool'), parts along dimension 1, may hold values from 0 to 4095, as said below
- query_pos: int32 [3, 32], P(None, 'groups'), parts along dimension 1, may hold values from 4096 to 8207
- lengths: int32 [32], P('groups'), parts along dimension 0, may hold values from 1024 to 4096, as said below
- query_weight: bfloat16 [8192, 8192], P('pool', 'heads'), may hold values from -0.0625 to 0.0625
- key_weight: bfloat16 [8192, 1024], P('pool', 'heads'), may hold values from -0.16503906 to 0.16503906
- value_weight: bfloat16 [8192, 1024], P('pool', 'heads'), may hold values from -0.16503906 to 0.16503906
- out_weight: bfloat16 [8192, 8192], P('heads', 'pool'), may hold values from -0.5 to 0.5
- gate_weight: bfloat16 [8192, 14848], P(None, ('pool', 'heads')), may hold values from -0.0625 to 0.0625
- up_weight: bfloat16 [8192, 14848], P(None, ('pool', 'heads')), may hold values from -0.0625 to 0.0625
- down_weight: bfloat16 [14848, 8192], P(('pool', 'heads')), may hold values from -0.0625 to 0.0625
Outputs:
- output: bfloat16 [32, 8192], P('groups', 'pool'), parts along dimension 0
There are 2 independent parts, one for each index of `groups`. A program takes and returns all parts, laid end to end along the dimension named above; an argument that names none is the same for every part. Nothing has to cross between parts.
Inputs may be any that keep to these rules, and one draw needn't show every extreme that they name: `positions`: text tokens carry three equal ids; one prompt is text only. `lengths`: some prompt fills all 4096 slots.
All inputs are finite; a program needn't handle non-finite values.
Results may differ from a plain program's by a relative error of at most 0.007.
The roundings to bfloat16 on the way count: a program that leaves them out, or rounds other values in their place, can miss the bound.
Values may be sent and summed in bfloat16 or wider, within the bound.
A program may use at most 192 MiB of HBM per device.

v0:
```python
import math
import jax
import jax.numpy as jnp
from jax import lax
from jax.sharding import PartitionSpec as P

D = 8192
HEADS = 64
KV_HEADS = 8
HD = 128
PROMPTS = 16
EPS = 1e-06
THETA = 1000000.0


def angle_tables(triple):
    half_dim = HD // 2
    column = jnp.arange(half_dim)
    first_end = HD // 8
    second_end = first_end + 3 * HD // 16
    chosen = jnp.where(
        column < first_end,
        triple[0][..., None],
        jnp.where(column < second_end, triple[1][..., None], triple[2][..., None]),
    )
    inverse = jnp.exp(column.astype(jnp.float32) * (-2.0 * math.log(THETA) / HD))
    angles = chosen.astype(jnp.float32) * inverse
    return (jnp.cos(angles), jnp.sin(angles))


def rotate(values, cos_table, sin_table):
    half_dim = values.shape[-1] // 2
    lower_half = values[..., :half_dim]
    upper_half = values[..., half_dim:]
    return jnp.concatenate(
        [
            lower_half * cos_table - upper_half * sin_table,
            upper_half * cos_table + lower_half * sin_table,
        ],
        -1,
    )


def normalize(values):
    return values * lax.rsqrt(jnp.mean(values * values, -1, keepdims=True) + EPS)


def prepare(projected_rows, item_ids, local_heads, query_pos):
    query_width = projected_rows.shape[1] - 2 * HD
    prompt_ids = item_ids // local_heads
    triple = query_pos[:, prompt_ids]
    cos_table, sin_table = angle_tables(triple)
    item_count = projected_rows.shape[0]
    raw_queries = projected_rows[:, :query_width].reshape(item_count, query_width // HD, HD)
    queries = rotate(raw_queries, cos_table[:, None], sin_table[:, None]).astype(jnp.bfloat16)
    own_keys = rotate(
        projected_rows[:, query_width : query_width + HD], cos_table, sin_table
    ).astype(jnp.bfloat16)
    own_values = projected_rows[:, query_width + HD :].astype(jnp.bfloat16)
    return (queries, own_keys, own_values)


def partial_softmax(queries, key_rows, value_rows, item_lengths, offset):
    scores = jnp.einsum(
        "igd,isd->igs", queries, key_rows, preferred_element_type=jnp.float32
    ) * HD ** (-0.5)
    slot_index = offset + jnp.arange(key_rows.shape[1])
    valid_mask = slot_index[None, None, :] < item_lengths[:, None, None]
    scores = jnp.where(valid_mask, scores, -1e30)
    peak_score = jnp.max(scores, -1)
    weights = jnp.where(valid_mask, jnp.exp(scores - peak_score[..., None]), 0.0)
    weighted = jnp.einsum("igs,isd->igd", weights, value_rows.astype(jnp.float32))
    return (peak_score, jnp.sum(weights, -1), weighted.reshape(queries.shape[0], -1))


def combine(peaks, totals, weighted, own_score, own_values):
    item_count, source_count, group_size = peaks.shape
    top_score = jnp.maximum(jnp.max(peaks, 1), own_score)
    factor = jnp.exp(peaks - top_score[:, None])
    own_weight = jnp.exp(own_score - top_score)
    denominator = jnp.sum(totals * factor, 1) + own_weight
    numerator = jnp.sum(
        weighted.reshape(item_count, source_count, group_size, HD) * factor[..., None], 1
    )
    numerator = numerator + own_weight[..., None] * own_values.astype(jnp.float32)[:, None, :]
    return (
        (numerator / denominator[..., None])
        .reshape(item_count, group_size * HD)
        .astype(jnp.bfloat16)
    )


def per_device(
    hidden_in,
    key_cache,
    value_cache,
    positions,
    query_pos,
    lengths,
    query_weight,
    key_weight,
    value_weight,
    out_weight,
    gate_weight,
    up_weight,
    down_weight,
):
    pool_index = lax.axis_index("pool")
    pool_size = lax.axis_size("pool")
    local_heads = key_cache.shape[1]
    group_size = HEADS // KV_HEADS
    query_width = group_size * HD
    all_items = PROMPTS * local_heads
    my_count = all_items // pool_size
    my_start = pool_index * my_count
    seq_local = key_cache.shape[2]
    block_cols = D // pool_size
    normed = normalize(hidden_in.astype(jnp.float32)).astype(jnp.bfloat16)
    normed_cols = lax.dynamic_slice_in_dim(normed, pool_index * block_cols, block_cols, 1)
    term = jnp.concatenate(
        [
            jnp.dot(normed_cols, query_weight, preferred_element_type=jnp.float32).reshape(
                PROMPTS, local_heads, query_width
            ),
            jnp.dot(normed_cols, key_weight, preferred_element_type=jnp.float32).reshape(
                PROMPTS, local_heads, HD
            ),
            jnp.dot(normed_cols, value_weight, preferred_element_type=jnp.float32).reshape(
                PROMPTS, local_heads, HD
            ),
        ],
        2,
    ).reshape(all_items, query_width + 2 * HD)
    cos_table, sin_table = angle_tables(positions)
    rotated = rotate(key_cache.astype(jnp.float32), cos_table[:, None], sin_table[:, None]).astype(
        jnp.bfloat16
    )
    rotated = rotated.reshape(all_items, seq_local, HD)
    value_rows = value_cache.reshape(all_items, seq_local, HD)
    item_lengths = jnp.repeat(lengths, local_heads)
    projected_all = lax.psum(term, "pool")
    all_queries, all_keys, all_values = prepare(
        projected_all, jnp.arange(all_items), local_heads, query_pos
    )
    local_peaks, local_totals, local_weighted = partial_softmax(
        all_queries, rotated, value_rows, item_lengths, pool_index * seq_local
    )
    peaks, totals, weighted = (
        lax.all_to_all(local_peaks[:, None], "pool", split_axis=0, concat_axis=1, tiled=True),
        lax.all_to_all(local_totals[:, None], "pool", split_axis=0, concat_axis=1, tiled=True),
        lax.all_to_all(local_weighted[:, None], "pool", split_axis=0, concat_axis=1, tiled=True),
    )
    queries = lax.dynamic_slice_in_dim(all_queries, my_start, my_count, 0)
    own_keys = lax.dynamic_slice_in_dim(all_keys, my_start, my_count, 0)
    own_values = lax.dynamic_slice_in_dim(all_values, my_start, my_count, 0)
    own_score = jnp.einsum(
        "igd,id->ig", queries, own_keys, preferred_element_type=jnp.float32
    ) * HD ** (-0.5)
    attended = combine(peaks, totals, weighted, own_score, own_values)
    gathered = lax.all_gather(attended, "pool", axis=0, tiled=True).reshape(
        PROMPTS, local_heads * query_width
    )
    attn_out = lax.psum(jnp.dot(gathered, out_weight, preferred_element_type=jnp.float32), "heads")
    hidden_cols = lax.dynamic_slice_in_dim(hidden_in, pool_index * block_cols, block_cols, 1)
    mid_state = (hidden_cols.astype(jnp.float32) + attn_out).astype(jnp.bfloat16)
    squares = lax.psum(jnp.sum(jnp.square(mid_state.astype(jnp.float32)), -1), "pool")
    whole_state = lax.all_gather(mid_state, "pool", axis=1, tiled=True)
    inverse = lax.rsqrt(squares / D + EPS)
    normed_state = (whole_state.astype(jnp.float32) * inverse[:, None]).astype(jnp.bfloat16)
    gate_values = jnp.dot(normed_state, gate_weight, preferred_element_type=jnp.float32)
    up_values = jnp.dot(normed_state, up_weight, preferred_element_type=jnp.float32)
    active = (jax.nn.silu(gate_values) * up_values).astype(jnp.bfloat16)
    partial_out = jnp.dot(active, down_weight, preferred_element_type=jnp.float32)
    mlp_cols = lax.psum_scatter(partial_out, "pool", scatter_dimension=1, tiled=True)
    mlp_cols = lax.psum(mlp_cols, "heads")
    return (mid_state.astype(jnp.float32) + mlp_cols).astype(jnp.bfloat16)


def solution(mesh):
    in_specs = (
        P("groups", None),
        P("groups", "heads", "pool", None),
        P("groups", "heads", "pool", None),
        P(None, "groups", "pool"),
        P(None, "groups"),
        P("groups"),
        P("pool", "heads"),
        P("pool", "heads"),
        P("pool", "heads"),
        P("heads", "pool"),
        P(None, ("pool", "heads")),
        P(None, ("pool", "heads")),
        P(("pool", "heads"), None),
    )
    out_specs = P("groups", "pool")
    return jax.shard_map(
        per_device, mesh=mesh, in_specs=in_specs, out_specs=out_specs, check_vma=False
    )
```

profile of v0, /device:TPU:0, one launch (start us, length us, event | category | flops | bytes accessed | tf_op | source)
XLA Modules:
  0.0 357.5 jit_solution(8407712216756091066)
XLA Ops:
  6.5 0.0 copy-start
  6.5 0.0 all-reduce.4.cloned.1.call-start
  6.5 1.1 convert_element_type.78
  7.6 1.1 multiply_reduce_fusion
  8.8 0.0 copy-done
  8.8 0.3 fusion.54
  9.1 1.5 fusion.50
  10.6 4.6 %fusion.52 = f32[16,4096]{1,0:T(8,128)S(1)} fusion(bf16[1024,4096]{1,0:T(8,128)(2,1)} %param.19, f32[16,8192]{1,0:T(8,128)S(1)} %convert_element_type.78, s32[]{:T(128)S(6)} %select_n.82, f32[16]{0:T(128)S(1)} %add_rsqrt_fusion.1), kind=kOutput, calls=%fused_computation.96 | convolution fusion | flops 134250496 | bytes 8716804 | tf_op jit(solution)/shard_map/dot_general | solution.py:122
  15.2 0.1 concatenate.27
  15.3 0.7 pad_maximum_fusion
  16.0 0.0 all-reduce.4.cloned.1.call-update
  16.1 0.0 copy-start.2
  16.1 0.0 copy-start.3
  16.1 0.0 copy-start.4
  16.1 11.3 %convert_element_type.82 = f32[16,4,512,128]{3,2,1,0:T(8,128)} convert(bf16[16,4,512,128]{3,2,1,0:T(8,128)(2,1)} %param.14) | non-fusion elementwise | flops 4194304 | bytes 25165824 | tf_op jit(solution)/shard_map/convert_element_type | solution.py:135
  27.5 0.0 copy-done.2
  27.5 0.1 copy.22
  27.6 0.6 gather_fusion
  28.2 0.2 slice_reduce_fusion.2
  28.4 0.0 copy-done.4
  28.4 0.1 broadcast_in_dim.119
  28.5 0.1 lt.54
  28.5 42.2 %fusion.5 = (f32[16,512,64]{2,1,0:T(8,128)S(1)}, f32[16,512,64]{2,1,0:T(8,128)S(1)}) fusion(f32[64]{0:T(128)S(1)} %multiply_exponential_fusion, s32[16,512]{1,0:T(8,128)S(1)} %get-tuple-element.23, s32[16,512]{1,0:T(8,128)S(1)} %get-tuple-element.24, s32[16,512]{1,0:T(8,128)S(1)} %get-tuple-element.22, pred[64]{0:T(512)(128)(4,1)S(1)} %get-tuple-element.29, ...), kind=kLoop, calls=%fused_computation.9 | loop fusion | flops 2097152 | bytes 4292992 | tf_op jit(solution)/shard_map/cos | solution.py:28
  70.7 19.2 %subtract_convert_fusion = (bf16[16,4,512,64]{3,2,1,0:T(8,128)(2,1)}, bf16[16,4,512,64]{3,2,1,0:T(8,128)(2,1)}) fusion(f32[16,4,512,128]{3,2,1,0:T(8,128)} %convert_element_type.82, f32[16,512,64]{2,1,0:T(8,128)S(1)} %get-tuple-element.21, f32[16,512,64]{2,1,0:T(8,128)S(1)} %get-tuple-element.20), kind=kLoop, calls=%fused_computation.2 | loop fusion | flops 16777216 | bytes 29360128 | tf_op jit(solution)/shard_map/convert.6
  90.0 0.1 broadcast_compare_fusion
  90.1 0.2 all-reduce.4.cloned.1.call-done
  90.3 1.0 slice_bitcast_fusion
  91.3 1.1 subtract_convert_fusion.2
  92.4 0.2 subtract_convert_fusion.1
  92.6 9.3 %fusion.49 = (f32[64,8]{1,0:T(8,128)}, f32[64,8,512]{2,1,0:T(8,128)S(1)}) fusion(bf16[64,512,64]{2,1,0:T(8,128)(2,1)} %bitcast.54, bf16[64,512,64]{2,1,0:T(8,128)(2,1)} %bitcast.53, bf16[64,8,64]{2,1,0:T(8,128)(2,1)S(1)} %get-tuple-element.19, bf16[64,8,64]{2,1,0:T(8,128)(2,1)S(1)} %get-tuple-element.18, pred[64,512]{1,0:T(8,128)(4,1)S(1)} %broadcast_compare_fusion), kind=kOutput, calls=%fused_computation.94 | convolution fusion | flops 84934144 | bytes 9603072 | tf_op jit(solution)/shard_map/igd,isd->igs/dot_general | solution.py:64
  101.9 7.1 %all-to-all-start.1 = ((f32[64,1,8]{2,1,0:T(1,128)}), f32[64,1,8]{2,1,0:T(1,128)S(1)}, u32[]{:S(2)}, u32[]{:S(2)}) async-start(f32[64,1,8]{2,1,0:T(1,128)} %bitcast.11), calls=%async_computation.1 | async-start | bytes 65536 | tf_op jit(solution)/shard_map/all_to_all | solution.py:149
  108.9 0.1 fusion.41
  109.0 0.2 fusion.36
  109.2 5.4 %fusion.14 = f32[64,8,128]{2,1,0:T(8,128)} fusion(bf16[64,512,128]{2,1,0:T(8,128)(2,1)} %bitcast.55, f32[64,8,512]{2,1,0:T(8,128)S(1)} %get-tuple-element.28, f32[64,8]{1,0:T(8,128)} %get-tuple-element.27, pred[64,512]{1,0:T(8,128)(4,1)S(1)} %broadcast_compare_fusion), kind=kOutput, calls=%fused_computation.16 | convolution fusion | flops 67633152 | bytes 9734144 | tf_op jit(solution)/shard_map/igs,isd->igd/dot_general | solution.py:72
  114.5 1.7 fusion.13
  116.3 0.8 slice.72
  117.1 0.0 all-to-all-done.1
  117.1 6.0 %all-to-all-start.2 = ((f32[64,1,8]{2,1,0:T(1,128)}), f32[64,1,8]{2,1,0:T(1,128)S(1)}, u32[]{:S(2)}, u32[]{:S(2)}) async-start(f32[64,1,8]{2,1,0:T(1,128)} %bitcast.21), calls=%async_computation.2 | async-start | bytes 65536 | tf_op jit(solution)/shard_map/all_to_all | solution.py:150
  123.1 6.7 %all-to-all-done.2 = f32[64,1,8]{2,1,0:T(1,128)S(1)} async-done(((f32[64,1,8]{2,1,0:T(1,128)}), f32[64,1,8]{2,1,0:T(1,128)S(1)}, u32[]{:S(2)}, u32[]{:S(2)}) %all-to-all-start.2) | async-done | bytes 2080 | tf_op jit(solution)/shard_map/all_to_all | solution.py:150
  129.7 3.4 all-to-all-start
  133.2 0.0 all-reduce.6.cloned.1.call-start
  133.3 0.1 copy.25
  133.3 0.1 copy.24
  133.4 7.9 %all-to-all-done = f32[64,1,1024]{2,1,0:T(1,128)S(1)} async-done(((f32[64,1,1024]{2,1,0:T(1,128)}), f32[64,1,1024]{2,1,0:T(1,128)S(1)}, u32[]{:S(2)}, u32[]{:S(2)}) %all-to-all-start) | async-done | bytes 262176 | tf_op jit(solution)/shard_map/all_to_all | solution.py:151
  141.3 0.1 mul.222
  141.4 0.4 multiply_reduce_fusion.1
  141.8 0.1 fusion.31
  141.9 30.6 %all_gather.6 = bf16[64,1024]{1,0:T(8,128)(2,1)S(1)} all-gather(bf16[8,1024]{1,0:T(8,128)(2,1)S(1)} %fusion.31), channel_id=1, replica_groups=mesh['groups'=2,'pool'=8,'heads'=2] {'pool'}, dimensions={0}, use_global_device_ids=true | all-gather | bytes 147456 | tf_op jit(solution)/shard_map/all_gather | solution.py:160
  172.5 0.1 reshape.304
  172.6 5.2 %fusion.56 = f32[16,1024]{1,0:T(8,128)} fusion(bf16[16,4096]{1,0:T(8,128)(2,1)S(1)} %reshape.304, bf16[4096,1024]{1,0:T(8,128)(2,1)} %param.22), kind=kOutput, calls=%fused_computation.98 | convolution fusion | flops 134217728 | bytes 8585216 | tf_op jit(solution)/shard_map/dot_general | solution.py:163
  177.8 0.0 all-reduce.6.cloned.1.call-update
  177.8 0.0 reduce-scatter.2.cloned.1.call-start
  177.8 16.1 %all-reduce.6.cloned.1.call-done = f32[16,1024]{1,0:T(8,128)} async-done(((f32[16,1024]{1,0:T(8,128)}), f32[16,1024]{1,0:T(8,128)}) %all-reduce.6.cloned.1.call-update) | async-done | bytes 65552 | tf_op jit(solution)/shard_map/psum | solution.py:163
  193.9 1.0 fusion.23
  194.9 31.1 %all_gather.7 = bf16[16,8192]{1,0:T(8,128)(2,1)S(1)} all-gather(bf16[16,1024]{1,0:T(8,128)(2,1)S(1)} %get-tuple-element.9), channel_id=1, replica_groups=mesh['groups'=2,'pool'=8,'heads'=2] {'pool'}, dimensions={1}, use_global_device_ids=true | all-gather | bytes 294912 | tf_op jit(solution)/shard_map/all_gather | solution.py:167
  226.0 21.3 %psum.30 = f32[16]{0:T(128)S(1)} all-reduce(f32[16]{0:T(128)S(1)} %get-tuple-element.8), channel_id=1, replica_groups=mesh['groups'=2,'pool'=8,'heads'=2] {'pool'}, use_global_device_ids=true, to_apply=%region_9.10 | all-reduce | flops 16 | bytes 128 | tf_op jit(solution)/shard_map/psum | solution.py:166
  247.3 9.4 %fusion.22 = f32[16,928]{1,0:T(8,128)S(1)} fusion(bf16[8192,928]{0,1:T(8,128)(2,1)} %param.23, bf16[16,8192]{1,0:T(8,128)(2,1)S(1)} %all_gather.7, f32[16]{0:T(128)S(1)} %add_rsqrt_fusion), kind=kOutput, calls=%fused_computation.33 | convolution fusion | flops 243662848 | bytes 15525952 | tf_op jit(solution)/shard_map/dot_general | solution.py:170
  256.7 13.9 %fusion.15 = f32[16,8192]{1,0:T(8,128)} fusion(bf16[928,8192]{1,0:T(8,128)(2,1)} %param.25, bf16[8192,928]{0,1:T(8,128)(2,1)} %param.24, bf16[16,8192]{1,0:T(8,128)(2,1)S(1)} %all_gather.7, f32[16]{0:T(128)S(1)} %add_rsqrt_fusion, f32[16,928]{1,0:T(8,128)S(1)} %fusion.22), kind=kOutput, calls=%fused_computation.17 | convolution fusion | flops 487021568 | bytes 31254592 | tf_op jit(solution)/shard_map/dot_general | solution.py:173
  270.6 0.0 reduce-scatter.2.cloned.1.call-update
  270.7 0.0 all-reduce.8.cloned.1.call-start
  270.7 60.0 %reduce-scatter.2.cloned.1.call-done = f32[16,1024]{1,0:T(8,128)} async-done(((f32[16,8192]{1,0:T(8,128)}), f32[16,1024]{1,0:T(8,128)}) %reduce-scatter.2.cloned.1.call-update) | async-done | bytes 65552 | tf_op jit(solution)/shard_map/reduce_scatter | solution.py:174
  330.7 0.0 all-reduce.8.cloned.1.call-update
  330.7 18.8 %all-reduce.8.cloned.1.call-done = f32[16,1024]{1,0:T(8,128)} async-done(((f32[16,1024]{1,0:T(8,128)}), f32[16,1024]{1,0:T(8,128)}) %all-reduce.8.cloned.1.call-update) | async-done | bytes 65552 | tf_op jit(solution)/shard_map/psum | solution.py:175
  349.5 1.5 fusion.24
  (19 shorter events, 0.2 us)
Async XLA Ops:
  6.5 2.2 copy-start
  6.5 83.8 %all-reduce.4.cloned.1.call-start = ((), (), s32[]{:S(2)}) async-start(), calls=%async_computation.4 | async-start | bytes 655360 | tf_op jit(solution)/shard_map/psum | solution.py:141
  16.1 11.4 %copy-start.2 = (s32[3,16,512]{2,1,0:T(8,128)S(1)}, s32[3,16,512]{2,1,0:T(8,128)}, u32[]{:S(2)}) copy-start(s32[3,16,512]{2,1,0:T(8,128)} %param.16) | copy-start | bytes 294916
  16.1 11.4 %copy-start.3 = (s32[3,16]{1,0:T(4,128)S(1)}, s32[3,16]{1,0:T(4,128)}, u32[]{:S(2)}) copy-start(s32[3,16]{1,0:T(4,128)} %param.17) | copy-start | bytes 580
  16.1 12.2 %copy-start.4 = (s32[16]{0:T(128)S(1)}, s32[16]{0:T(128)}, u32[]{:S(2)}) copy-start(s32[16]{0:T(128)} %param.18) | copy-start | bytes 196
  101.9 15.2 %all-to-all-start.1 = ((f32[64,1,8]{2,1,0:T(1,128)}), f32[64,1,8]{2,1,0:T(1,128)S(1)}, u32[]{:S(2)}, u32[]{:S(2)}) async-start(f32[64,1,8]{2,1,0:T(1,128)} %bitcast.11), calls=%async_computation.1 | async-start | bytes 65536 | tf_op jit(solution)/shard_map/all_to_all | solution.py:149
  117.1 12.7 %all-to-all-start.2 = ((f32[64,1,8]{2,1,0:T(1,128)}), f32[64,1,8]{2,1,0:T(1,128)S(1)}, u32[]{:S(2)}, u32[]{:S(2)}) async-start(f32[64,1,8]{2,1,0:T(1,128)} %bitcast.21), calls=%async_computation.2 | async-start | bytes 65536 | tf_op jit(solution)/shard_map/all_to_all | solution.py:150
  129.7 11.6 %all-to-all-start = ((f32[64,1,1024]{2,1,0:T(1,128)}), f32[64,1,1024]{2,1,0:T(1,128)S(1)}, u32[]{:S(2)}, u32[]{:S(2)}) async-start(f32[64,1,1024]{2,1,0:T(1,128)} %bitcast.8), calls=%async_computation | async-start | bytes 524288 | tf_op jit(solution)/shard_map/all_to_all | solution.py:151
  133.2 60.8 %all-reduce.6.cloned.1.call-start = ((), (), s32[]{:S(2)}) async-start(), calls=%async_computation.5 | async-start | bytes 131072 | tf_op jit(solution)/shard_map/psum | solution.py:163
  177.8 152.9 %reduce-scatter.2.cloned.1.call-start = ((), (), s32[]{:S(2)}) async-start(), calls=%async_computation.6 | async-start | bytes 589824 | tf_op jit(solution)/shard_map/reduce_scatter | solution.py:174
  247.3 103.7 %copy-start.1 = (bf16[1024,512]{1,0:T(8,128)(2,1)S(1)}, bf16[1024,512]{1,0:T(8,128)(2,1)}, u32[]{:S(2)}) copy-start(bf16[1024,512]{1,0:T(8,128)(2,1)} %param.21) | copy-start | bytes 3145732
  270.7 78.9 %all-reduce.8.cloned.1.call-start = ((), (), s32[]{:S(2)}) async-start(), calls=%async_computation.7 | async-start | bytes 131072 | tf_op jit(solution)/shard_map/psum | solution.py:175
Sparse Core Ops, SparseCore 0:
  16.2 74.0 all-reduce.3
  177.9 15.9 all-reduce.5
  270.8 59.8 reduce-scatter.1
  332.8 16.6 all-reduce.7
where the time goes:
time: 358 us
  waiting for transfers between devices  110 us (31%)
  blocking collectives  82.9 us (23%)
  other arithmetic  81.8 us (23%)
  matrix products  49.8 us (14%)
  starting transfers between devices  16.6 us (5%)
  between operations  13.3 us (4%)
    reduce_scatter x1, waiting for transfers between devices, per_device(): lax.psum_scatter(partial_out, 'pool', scatter_dimension=1, tiled=True)  60 us
    cos x1, other arithmetic, angle_tables(): return (jnp.cos(angles), jnp.sin(angles))  42.2 us
    all_gather x1, blocking collectives, per_device(): whole_state = lax.all_gather(mid_state, 'pool', axis=1, tiled=True)  31.1 us
    all_gather x1, blocking collectives, per_device(): lax.all_gather(attended, 'pool', axis=0, tiled=True)  30.6 us
    psum x1, blocking collectives, per_device(): lax.psum(jnp.sum(jnp.square(mid_state.astype(jnp.float32)), -1), 'pool')  21.3 us
    another operation x3, other arithmetic  20.5 us
    psum x1, waiting for transfers between devices, per_device(): mlp_cols = lax.psum(mlp_cols, 'heads')  18.8 us
    psum x1, waiting for transfers between devices, per_device(): lax.psum(jnp.dot(gathered, out_weight, preferred_element_type=jnp.float32...  16.1 us
  transfers between devices with their start and end apart: 7, of which 6 were waited for; matrix products, arithmetic and copies ran while one was open for 23% of the time, Pallas kernels for 0%

commit v1 on v0

--- a/solution.py
+++ b/solution.py
@@ -172,7 +172,7 @@
     active = (jax.nn.silu(gate_values) * up_values).astype(jnp.bfloat16)
     partial_out = jnp.dot(active, down_weight, preferred_element_type=jnp.float32)
     mlp_cols = lax.psum_scatter(partial_out, "pool", scatter_dimension=1, tiled=True)
-    mlp_cols = lax.psum(mlp_cols, "heads")
+    mlp_cols = jnp.sum(lax.all_gather(mlp_cols, "heads"), axis=0)
     return (mid_state.astype(jnp.float32) + mlp_cols).astype(jnp.bfloat16)
 
 

time: 358 us -> 341 us (0.953)
  waiting for transfers between devices: 110 us -> 91 us
    psum x1 -> x0, waiting for transfers between devices: 18.8 us -> none  [per_device(): mlp_cols = lax.psum(mlp_cols, 'heads')]
  transfers between devices with their start and end apart: 7 -> 6, of which waited for: 6 -> 5; matrix products, arithmetic and copies ran while one was open for 23% -> 24% of each run, Pallas kernels for 0% -> 0%
where the time goes in v1:
time: 341 us; the launch traced here: 340 us
  waiting for transfers between devices  91 us (27%)
  blocking collectives  85 us (25%)
  other arithmetic  81 us (24%)
  matrix products  49.8 us (15%)
  starting transfers between devices  16.6 us (5%)
  between operations  13.3 us (4%)
    reduce_scatter x1, waiting for transfers between devices, per_device(): lax.psum_scatter(partial_out, 'pool', scatter_dimension=1, tiled=True)  60 us
    cos x1, other arithmetic, angle_tables(): return (jnp.cos(angles), jnp.sin(angles))  42.2 us
    all_gather x1, blocking collectives, per_device(): whole_state = lax.all_gather(mid_state, 'pool', axis=1, tiled=True)  31.1 us
    all_gather x1, blocking collectives, per_device(): lax.all_gather(attended, 'pool', axis=0, tiled=True)  30.6 us
    psum x1, blocking collectives, per_device(): lax.psum(jnp.sum(jnp.square(mid_state.astype(jnp.float32)), -1), 'pool')  21.3 us
    another operation x3, other arithmetic  20.5 us
    psum x1, waiting for transfers between devices, per_device(): lax.psum(jnp.dot(gathered, out_weight, preferred_element_type=jnp.float32...  16.1 us
    dot_general x1, matrix products, per_device(): jnp.dot(active, down_weight, preferred_element_type=jnp.float32)  13.9 us
  transfers between devices with their start and end apart: 6, of which 5 were waited for; matrix products, arithmetic and copies ran while one was open for 24% of the time, Pallas kernels for 0%

profile of v1, /device:TPU:0, one launch (start us, length us, event | category | flops | bytes accessed | tf_op | source)
XLA Modules:
  0.0 339.9 jit_solution(11020386325790482395)
XLA Ops:
  6.5 0.0 copy-start
  6.5 0.0 all-reduce.3.cloned.1.call-start
  6.5 1.1 convert_element_type.78
  7.6 1.1 multiply_reduce_fusion
  8.8 0.0 copy-done
  8.8 0.3 fusion.54
  9.1 1.5 fusion.50
  10.6 4.6 %fusion.52 = f32[16,4096]{1,0:T(8,128)S(1)} fusion(bf16[1024,4096]{1,0:T(8,128)(2,1)} %param.19, f32[16,8192]{1,0:T(8,128)S(1)} %convert_element_type.78, s32[]{:T(128)S(6)} %select_n.82, f32[16]{0:T(128)S(1)} %add_rsqrt_fusion.1), kind=kOutput, calls=%fused_computation.96 | convolution fusion | flops 134250496 | bytes 8716804 | tf_op jit(solution)/shard_map/dot_general | solution.py:122
  15.2 0.1 concatenate.27
  15.3 0.7 pad_maximum_fusion
  16.0 0.0 all-reduce.3.cloned.1.call-update
  16.1 0.0 copy-start.2
  16.1 0.0 copy-start.3
  16.1 0.0 copy-start.4
  16.1 11.3 %convert_element_type.82 = f32[16,4,512,128]{3,2,1,0:T(8,128)} convert(bf16[16,4,512,128]{3,2,1,0:T(8,128)(2,1)} %param.14) | non-fusion elementwise | flops 4194304 | bytes 25165824 | tf_op jit(solution)/shard_map/convert_element_type | solution.py:135
  27.5 0.0 copy-done.2
  27.5 0.0 copy-done.3
  27.5 0.1 copy.22
  27.6 0.6 gather_fusion
  28.2 0.2 slice_reduce_fusion.2
  28.4 0.0 copy-done.4
  28.4 0.1 broadcast_in_dim.119
  28.5 0.1 lt.54
  28.5 42.2 %fusion.5 = (f32[16,512,64]{2,1,0:T(8,128)S(1)}, f32[16,512,64]{2,1,0:T(8,128)S(1)}) fusion(f32[64]{0:T(128)S(1)} %multiply_exponential_fusion, s32[16,512]{1,0:T(8,128)S(1)} %get-tuple-element.23, s32[16,512]{1,0:T(8,128)S(1)} %get-tuple-element.24, s32[16,512]{1,0:T(8,128)S(1)} %get-tuple-element.22, pred[64]{0:T(512)(128)(4,1)S(1)} %get-tuple-element.29, ...), kind=kLoop, calls=%fused_computation.9 | loop fusion | flops 2097152 | bytes 4292992 | tf_op jit(solution)/shard_map/cos | solution.py:28
  70.7 19.2 %subtract_convert_fusion = (bf16[16,4,512,64]{3,2,1,0:T(8,128)(2,1)}, bf16[16,4,512,64]{3,2,1,0:T(8,128)(2,1)}) fusion(f32[16,4,512,128]{3,2,1,0:T(8,128)} %convert_element_type.82, f32[16,512,64]{2,1,0:T(8,128)S(1)} %get-tuple-element.21, f32[16,512,64]{2,1,0:T(8,128)S(1)} %get-tuple-element.20), kind=kLoop, calls=%fused_computation.2 | loop fusion | flops 16777216 | bytes 29360128 | tf_op jit(solution)/shard_map/convert.6
  90.0 0.1 broadcast_compare_fusion
  90.1 0.2 all-reduce.3.cloned.1.call-done
  90.3 1.0 slice_bitcast_fusion
  91.3 1.1 subtract_convert_fusion.2
  92.4 0.2 subtract_convert_fusion.1
  92.6 9.3 %fusion.49 = (f32[64,8]{1,0:T(8,128)}, f32[64,8,512]{2,1,0:T(8,128)S(1)}) fusion(bf16[64,512,64]{2,1,0:T(8,128)(2,1)} %bitcast.55, bf16[64,512,64]{2,1,0:T(8,128)(2,1)} %bitcast.54, bf16[64,8,64]{2,1,0:T(8,128)(2,1)S(1)} %get-tuple-element.19, bf16[64,8,64]{2,1,0:T(8,128)(2,1)S(1)} %get-tuple-element.18, pred[64,512]{1,0:T(8,128)(4,1)S(1)} %broadcast_compare_fusion), kind=kOutput, calls=%fused_computation.94 | convolution fusion | flops 84934144 | bytes 9603072 | tf_op jit(solution)/shard_map/igd,isd->igs/dot_general | solution.py:64
  101.9 7.1 %all-to-all-start.1 = ((f32[64,1,8]{2,1,0:T(1,128)}), f32[64,1,8]{2,1,0:T(1,128)S(1)}, u32[]{:S(2)}, u32[]{:S(2)}) async-start(f32[64,1,8]{2,1,0:T(1,128)} %bitcast.11), calls=%async_computation.1 | async-start | bytes 65536 | tf_op jit(solution)/shard_map/all_to_all | solution.py:149
  108.9 0.1 fusion.41
  109.0 0.2 fusion.36
  109.2 5.4 %fusion.14 = f32[64,8,128]{2,1,0:T(8,128)} fusion(bf16[64,512,128]{2,1,0:T(8,128)(2,1)} %bitcast.56, f32[64,8,512]{2,1,0:T(8,128)S(1)} %get-tuple-element.28, f32[64,8]{1,0:T(8,128)} %get-tuple-element.27, pred[64,512]{1,0:T(8,128)(4,1)S(1)} %broadcast_compare_fusion), kind=kOutput, calls=%fused_computation.16 | convolution fusion | flops 67633152 | bytes 9734144 | tf_op jit(solution)/shard_map/igs,isd->igd/dot_general | solution.py:72
  114.5 1.7 fusion.13
  116.3 0.8 slice.72
  117.1 0.0 all-to-all-done.1
  117.1 6.0 %all-to-all-start.2 = ((f32[64,1,8]{2,1,0:T(1,128)}), f32[64,1,8]{2,1,0:T(1,128)S(1)}, u32[]{:S(2)}, u32[]{:S(2)}) async-start(f32[64,1,8]{2,1,0:T(1,128)} %bitcast.21), calls=%async_computation.2 | async-start | bytes 65536 | tf_op jit(solution)/shard_map/all_to_all | solution.py:150
  123.1 6.7 %all-to-all-done.2 = f32[64,1,8]{2,1,0:T(1,128)S(1)} async-done(((f32[64,1,8]{2,1,0:T(1,128)}), f32[64,1,8]{2,1,0:T(1,128)S(1)}, u32[]{:S(2)}, u32[]{:S(2)}) %all-to-all-start.2) | async-done | bytes 2080 | tf_op jit(solution)/shard_map/all_to_all | solution.py:150
  129.7 3.4 %all-to-all-start = ((f32[64,1,1024]{2,1,0:T(1,128)}), f32[64,1,1024]{2,1,0:T(1,128)S(1)}, u32[]{:S(2)}, u32[]{:S(2)}) async-start(f32[64,1,1024]{2,1,0:T(1,128)} %bitcast.8), calls=%async_computation | async-start | bytes 524288 | tf_op jit(solution)/shard_map/all_to_all | solution.py:151
  133.2 0.0 all-reduce.5.cloned.1.call-start
  133.3 0.1 copy.25
  133.3 0.1 copy.24
  133.4 7.9 %all-to-all-done = f32[64,1,1024]{2,1,0:T(1,128)S(1)} async-done(((f32[64,1,1024]{2,1,0:T(1,128)}), f32[64,1,1024]{2,1,0:T(1,128)S(1)}, u32[]{:S(2)}, u32[]{:S(2)}) %all-to-all-start) | async-done | bytes 262176 | tf_op jit(solution)/shard_map/all_to_all | solution.py:151
  141.3 0.1 mul.222
  141.4 0.4 multiply_reduce_fusion.1
  141.8 0.1 fusion.31
  141.9 30.6 %all_gather.12 = bf16[64,1024]{1,0:T(8,128)(2,1)S(1)} all-gather(bf16[8,1024]{1,0:T(8,128)(2,1)S(1)} %fusion.31), channel_id=1, replica_groups=mesh['groups'=2,'pool'=8,'heads'=2] {'pool'}, dimensions={0}, use_global_device_ids=true | all-gather | bytes 147456 | tf_op jit(solution)/shard_map/all_gather | solution.py:160
  172.5 0.1 reshape.304
  172.6 5.2 %fusion.56 = f32[16,1024]{1,0:T(8,128)} fusion(bf16[16,4096]{1,0:T(8,128)(2,1)S(1)} %reshape.304, bf16[4096,1024]{1,0:T(8,128)(2,1)} %param.22), kind=kOutput, calls=%fused_computation.98 | convolution fusion | flops 134217728 | bytes 8585216 | tf_op jit(solution)/shard_map/dot_general | solution.py:163
  177.8 0.0 all-reduce.5.cloned.1.call-update
  177.8 0.0 reduce-scatter.2.cloned.1.call-start
  177.8 16.1 %all-reduce.5.cloned.1.call-done = f32[16,1024]{1,0:T(8,128)} async-done(((f32[16,1024]{1,0:T(8,128)}), f32[16,1024]{1,0:T(8,128)}) %all-reduce.5.cloned.1.call-update) | async-done | bytes 65552 | tf_op jit(solution)/shard_map/psum | solution.py:163
  193.9 1.0 fusion.23
  194.9 31.1 %all_gather.13 = bf16[16,8192]{1,0:T(8,128)(2,1)S(1)} all-gather(bf16[16,1024]{1,0:T(8,128)(2,1)S(1)} %get-tuple-element.9), channel_id=1, replica_groups=mesh['groups'=2,'pool'=8,'heads'=2] {'pool'}, dimensions={1}, use_global_device_ids=true | all-gather | bytes 294912 | tf_op jit(solution)/shard_map/all_gather | solution.py:167
  226.0 21.3 %psum.23 = f32[16]{0:T(128)S(1)} all-reduce(f32[16]{0:T(128)S(1)} %get-tuple-element.8), channel_id=1, replica_groups=mesh['groups'=2,'pool'=8,'heads'=2] {'pool'}, use_global_device_ids=true, to_apply=%region_9.10 | all-reduce | flops 16 | bytes 128 | tf_op jit(solution)/shard_map/psum | solution.py:166
  247.3 9.4 %fusion.22 = f32[16,928]{1,0:T(8,128)S(1)} fusion(bf16[8192,928]{0,1:T(8,128)(2,1)} %param.23, bf16[16,8192]{1,0:T(8,128)(2,1)S(1)} %all_gather.13, f32[16]{0:T(128)S(1)} %add_rsqrt_fusion), kind=kOutput, calls=%fused_computation.33 | convolution fusion | flops 243662848 | bytes 15525952 | tf_op jit(solution)/shard_map/dot_general | solution.py:170
  256.7 13.9 %fusion.15 = f32[16,8192]{1,0:T(8,128)} fusion(bf16[928,8192]{1,0:T(8,128)(2,1)} %param.25, bf16[8192,928]{0,1:T(8,128)(2,1)} %param.24, bf16[16,8192]{1,0:T(8,128)(2,1)S(1)} %all_gather.13, f32[16]{0:T(128)S(1)} %add_rsqrt_fusion, f32[16,928]{1,0:T(8,128)S(1)} %fusion.22), kind=kOutput, calls=%fused_computation.17 | convolution fusion | flops 487021568 | bytes 31254592 | tf_op jit(solution)/shard_map/dot_general | solution.py:173
  270.6 0.0 reduce-scatter.2.cloned.1.call-update
  270.7 60.0 %reduce-scatter.2.cloned.1.call-done = f32[16,1024]{1,0:T(8,128)} async-done(((f32[16,8192]{1,0:T(8,128)}), f32[16,1024]{1,0:T(8,128)}) %reduce-scatter.2.cloned.1.call-update) | async-done | bytes 65552 | tf_op jit(solution)/shard_map/reduce_scatter | solution.py:174
  330.7 2.1 all-gather
  332.8 0.6 fusion.24
  333.4 0.0 copy-done.1
  (18 shorter events, 0.2 us)
Async XLA Ops:
  6.5 2.2 copy-start
  6.5 83.8 %all-reduce.3.cloned.1.call-start = ((), (), s32[]{:S(2)}) async-start(), calls=%async_computation.4 | async-start | bytes 655360 | tf_op jit(solution)/shard_map/psum | solution.py:141
  16.1 11.4 %copy-start.2 = (s32[3,16,512]{2,1,0:T(8,128)S(1)}, s32[3,16,512]{2,1,0:T(8,128)}, u32[]{:S(2)}) copy-start(s32[3,16,512]{2,1,0:T(8,128)} %param.16) | copy-start | bytes 294916
  16.1 11.4 %copy-start.3 = (s32[3,16]{1,0:T(4,128)S(1)}, s32[3,16]{1,0:T(4,128)}, u32[]{:S(2)}) copy-start(s32[3,16]{1,0:T(4,128)} %param.17) | copy-start | bytes 580
  16.1 12.2 %copy-start.4 = (s32[16]{0:T(128)S(1)}, s32[16]{0:T(128)}, u32[]{:S(2)}) copy-start(s32[16]{0:T(128)} %param.18) | copy-start | bytes 196
  101.9 15.2 %all-to-all-start.1 = ((f32[64,1,8]{2,1,0:T(1,128)}), f32[64,1,8]{2,1,0:T(1,128)S(1)}, u32[]{:S(2)}, u32[]{:S(2)}) async-start(f32[64,1,8]{2,1,0:T(1,128)} %bitcast.11), calls=%async_computation.1 | async-start | bytes 65536 | tf_op jit(solution)/shard_map/all_to_all | solution.py:149
  117.1 12.7 %all-to-all-start.2 = ((f32[64,1,8]{2,1,0:T(1,128)}), f32[64,1,8]{2,1,0:T(1,128)S(1)}, u32[]{:S(2)}, u32[]{:S(2)}) async-start(f32[64,1,8]{2,1,0:T(1,128)} %bitcast.21), calls=%async_computation.2 | async-start | bytes 65536 | tf_op jit(solution)/shard_map/all_to_all | solution.py:150
  129.7 11.6 %all-to-all-start = ((f32[64,1,1024]{2,1,0:T(1,128)}), f32[64,1,1024]{2,1,0:T(1,128)S(1)}, u32[]{:S(2)}, u32[]{:S(2)}) async-start(f32[64,1,1024]{2,1,0:T(1,128)} %bitcast.8), calls=%async_computation | async-start | bytes 524288 | tf_op jit(solution)/shard_map/all_to_all | solution.py:151
  133.2 60.8 %all-reduce.5.cloned.1.call-start = ((), (), s32[]{:S(2)}) async-start(), calls=%async_computation.5 | async-start | bytes 131072 | tf_op jit(solution)/shard_map/psum | solution.py:163
  177.8 152.9 %reduce-scatter.2.cloned.1.call-start = ((), (), s32[]{:S(2)}) async-start(), calls=%async_computation.6 | async-start | bytes 589824 | tf_op jit(solution)/shard_map/reduce_scatter | solution.py:174
  247.3 86.1 %copy-start.1 = (bf16[1024,512]{1,0:T(8,128)(2,1)S(1)}, bf16[1024,512]{1,0:T(8,128)(2,1)}, u32[]{:S(2)}) copy-start(bf16[1024,512]{1,0:T(8,128)(2,1)} %param.21) | copy-start | bytes 3145732
Sparse Core Ops, SparseCore 0:
  16.2 74.0 all-reduce.2
  177.9 15.9 all-reduce.4
  270.8 59.8 reduce-scatter.1
